TPU v7x, 32 devices: a whole 2x2x4 slice. The times are simulated.
32 devices in a mesh: grp: 2 (over y), tm: 4 (over z), chan: 2 (over x), sub: 2 (over core).
Axes of the slice: x: 2, y: 2, z: 4, core: 2. Of those that a mesh axis runs over, the one named last changes fastest.
Arguments:
- signal: float32 [64, 131072], P(('grp', 'chan', 'sub'), 'tm'), parts along dimension 0, may hold values from -24 to 24
- gap_mask: int32 [64, 8], P(('grp', 'chan', 'sub'), 'tm'), parts along dimension 0, may hold values from 0 to 1, as said below
- assignment: int32 [64], P(('grp', 'chan', 'sub')), parts along dimension 0, may hold values from 0 to 7, as said below
Outputs:
- peak_hold: float32 [64, 16384], P(('grp', 'chan', 'sub'), 'tm'), parts along dimension 0
- log_mean: float32 [64, 16384], P(('grp', 'chan', 'sub'), 'tm'), parts along dimension 0
- block_mean: float32 [16, 16384], P('grp', 'tm'), parts along dimension 0
There are 2 independent parts, one for each index of `grp`. A program takes and returns all parts, laid end to end along the dimension named above; each array names one. Nothing has to cross between parts.
Inputs may be any that keep to these rules, and one draw needn't show every extreme that they name: `gap_mask`: every channel keeps at least one of its 8 segments. `assignment`: every block holds at least one channel.
All inputs are finite; a program needn't handle non-finite values.
Results may differ from a plain program's by a relative error of at most 0.000086.
Values sent between devices are 32-bit elements; how exact they have to be, the bound alone decides.
A program may use at most 128 MiB of HBM per device.

v0:
```python
import math
import jax
import jax.numpy as jnp
from jax import lax
from jax.sharding import PartitionSpec as P

LA = 256
LB = 128
BLOCKS = 8


def from_behind(x, axis, by):
    count = lax.axis_size(axis)
    pairs = [(i, i + by) for i in range(count) if 0 <= i + by < count]
    return lax.ppermute(x, axis, pairs)


def rotations(height, columns, modulus):
    products = (
        jnp.arange(height, dtype=jnp.int32)[:, None]
        * jnp.arange(columns, dtype=jnp.int32)[None, :]
        % modulus
    )
    angles = products.astype(jnp.float32) * (2.0 * math.pi / modulus)
    return (jnp.cos(angles), -jnp.sin(angles))


def on_device(signal, gap_mask, assignment):
    channels, local_time = signal.shape
    seg_local = gap_mask.shape[1]
    half = local_time // seg_local
    seg_length = LA * LB
    highest = lax.Precision.HIGHEST
    borrowed = from_behind(signal[:, :half], "tm", -1)
    extended = jnp.concatenate([signal, borrowed], axis=1)
    hop_rows = extended.reshape(channels, seg_local + 1, half)
    section_one = rotations(LB, LB, LB)
    twiddle = rotations(LB, LA, seg_length)
    section_two = rotations(LA, LA // 2, LA)
    samples = jnp.arange(seg_length, dtype=jnp.float32)
    window = (0.5 - 0.5 * jnp.cos(samples * (2.0 * math.pi / seg_length))).reshape(LB, LA)
    norm_scale = 1.0 / (0.375 * seg_length)

    def one_channel(inputs):
        rows_here, keep_flags = inputs
        segments = jnp.concatenate([rows_here[:-1], rows_here[1:]], axis=-1)
        frames = segments.reshape(seg_local, LB, LA) * window
        real_one = jnp.einsum("kb,sba->ska", section_one[0], frames, precision=highest)
        imag_one = jnp.einsum("kb,sba->ska", section_one[1], frames, precision=highest)
        real_mid = real_one * twiddle[0] - imag_one * twiddle[1]
        imag_mid = real_one * twiddle[1] + imag_one * twiddle[0]
        real_two = jnp.einsum(
            "ska,aj->skj", real_mid, section_two[0], precision=highest
        ) - jnp.einsum("ska,aj->skj", imag_mid, section_two[1], precision=highest)
        imag_two = jnp.einsum(
            "ska,aj->skj", real_mid, section_two[1], precision=highest
        ) + jnp.einsum("ska,aj->skj", imag_mid, section_two[0], precision=highest)
        powers = (real_two * real_two + imag_two * imag_two) * norm_scale
        powers = jnp.swapaxes(powers, 1, 2).reshape(seg_local, -1)
        weights = keep_flags.astype(jnp.float32)
        peak_local = jnp.max(powers * weights[:, None], axis=0)
        log_terms = jnp.sum(weights[:, None] * jnp.log(0.25 + powers), axis=0)
        return (peak_local, log_terms)

    peak_local, log_terms = lax.map(one_channel, (hop_rows, gap_mask))
    kept_local = jnp.sum(gap_mask.astype(jnp.float32), axis=1)
    time_devices = lax.axis_size("tm")
    bin_width = peak_local.shape[1] // time_devices
    count_terms = jnp.broadcast_to(kept_local[:, None], (channels, time_devices))
    peak_all = lax.pmax(peak_local, "tm")
    peak_hold = lax.dynamic_slice_in_dim(peak_all, lax.axis_index("tm") * bin_width, bin_width, 1)
    log_sum, kept_total = (
        lax.psum_scatter(log_terms, "tm", scatter_dimension=1, tiled=True),
        lax.psum_scatter(count_terms, "tm", scatter_dimension=1, tiled=True),
    )
    log_mean = log_sum / kept_total
    onehot = (assignment[None, :] == jnp.arange(BLOCKS, dtype=jnp.int32)[:, None]).astype(
        jnp.float32
    )
    block_part = jnp.dot(onehot, log_mean, precision=highest)
    block_total, block_counts = lax.psum((block_part, jnp.sum(onehot, axis=1)), ("chan", "sub"))
    block_mean = block_total / block_counts[:, None]
    return (peak_hold, log_mean, block_mean)


def solution(mesh):
    in_specs = (
        P(("grp", "chan", "sub"), "tm"),
        P(("grp", "chan", "sub"), "tm"),
        P(("grp", "chan", "sub")),
    )
    out_specs = (P(("grp", "chan", "sub"), "tm"), P(("grp", "chan", "sub"), "tm"), P("grp", "tm"))
    return jax.shard_map(
        on_device, mesh=mesh, in_specs=in_specs, out_specs=out_specs, check_vma=False
    )
```

profile of v0, /device:TPU:0, one launch (start us, length us, event | category | flops | bytes accessed | tf_op | source)
XLA Modules:
  0.0 217.9 jit_solution(8996956551035906242)
XLA Ops:
  7.2 1.2 slice.11
  8.4 1.3 collective-permute-start
  10.5 14.9 %collective-permute-done = f32[8,16384]{1,0:T(8,128)} collective-permute-done((f32[8,16384]{1,0:T(8,128)S(1)}, f32[8,16384]{1,0:T(8,128)}, u32[]{:S(2)}, u32[]{:S(2)}) %collective-permute-start) | collective-permute-done | bytes 524320 | tf_op jit(solution)/shard_map/ppermute | solution.py:15
  25.4 1.1 pad_maximum_fusion
  26.5 2.5 %reshape.43 = f32[8,3,16384]{2,1,0:T(4,128)} reshape(f32[8,49152]{1,0:T(8,128)S(1)} %pad_maximum_fusion) | data formatting | bytes 3145728 | tf_op jit(solution)/shard_map/reshape | solution.py:36
  29.0 84.5 %while.14 = (s32[]{:T(128)}, f32[8,16384]{1,0:T(8,128)S(1)}, f32[8,16384]{1,0:T(8,128)}, f32[8,3,16384]{2,1,0:T(4,128)}, s32[8,2]{1,0:T(8,128)S(1)}, /*index=5*/s32[]{:T(128)}, s32[]{:T(128)}, s32[]{}) while((s32[]{:T(128)}, f32[8,16384]{1,0:T(8,128)S(1)}, f32[8,16384]{1,0:T(8,128)}, f32[8,3,16384]{2,1,0:T(4,128)}, ...), condition=%wide.region_3.4_spmd.clone.clone, body=%wide.region_0.3_spmd.clone.clone.sunk | while | flops 608321536 | bytes 8388765 | solution.py:65
  29.0 1.2 constant_dynamic-slice_fusion.5
  37.1 1.9 dynamic_update_slice.14
  39.6 1.1 constant_dynamic-slice_fusion.5
  47.6 1.9 dynamic_update_slice.14
  50.2 1.1 constant_dynamic-slice_fusion.5
  57.1 1.0 multiply_reduce_fusion.3
  58.2 1.9 dynamic_update_slice.14
  60.7 1.1 constant_dynamic-slice_fusion.5
  68.7 1.9 dynamic_update_slice.14
  71.3 1.1 constant_dynamic-slice_fusion.5
  78.2 1.0 multiply_reduce_fusion.3
  79.3 1.9 dynamic_update_slice.14
  81.9 1.1 constant_dynamic-slice_fusion.5
  89.9 1.9 dynamic_update_slice.14
  92.4 1.1 constant_dynamic-slice_fusion.5
  99.3 1.0 multiply_reduce_fusion.3
  100.4 1.9 dynamic_update_slice.14
  103.0 1.1 constant_dynamic-slice_fusion.5
  111.0 1.9 dynamic_update_slice.14
  113.7 5.9 %psum.15 = f32[8]{0:T(128)S(1)} all-reduce(f32[8]{0:T(128)S(1)} %convert_reduce_fusion), channel_id=1, replica_groups=mesh['grp'=2,'tm'=4,'chan'=2,'sub'=2] {'chan','sub'}, use_global_device_ids=true, to_apply=%region_10.11 | all-reduce | flops 8 | bytes 64 | tf_op jit(solution)/shard_map/psum | solution.py:81
  120.2 10.0 %all-reduce = f32[8,4]{0,1:T(4,128)S(1)} all-reduce(f32[8,4]{0,1:T(4,128)S(1)} %broadcast_in_dim.8), channel_id=3, replica_groups=mesh['grp'=2,'tm'=4,'chan'=2,'sub'=2] {'tm'}, use_global_device_ids=true, to_apply=%region_7.8.clone | all-reduce | flops 32 | bytes 256
  131.0 5.0 %reduce-scatter.2.cloned.1.call-done = f32[8,4096]{1,0:T(8,128)} async-done(((f32[8,16384]{1,0:T(8,128)}), f32[8,4096]{1,0:T(8,128)}) %reduce-scatter.2.cloned.1.call-update) | async-done | bytes 131088 | tf_op jit(solution)/shard_map/reduce_scatter | solution.py:73
  137.9 37.3 %all-reduce.4.cloned.1.call-done = f32[8,16384]{1,0:T(8,128)} async-done(((f32[8,16384]{1,0:T(8,128)}), f32[8,16384]{1,0:T(8,128)}) %all-reduce.4.cloned.1.call-update) | async-done | bytes 524304 | tf_op jit(solution)/shard_map/pmax | solution.py:70
  175.2 1.6 constant_dynamic-slice_fusion.3
  176.8 32.9 %all-reduce.6.cloned.1.call-done = f32[8,4096]{1,0:T(8,128)} async-done(((f32[8,4096]{1,0:T(8,128)}), f32[8,4096]{1,0:T(8,128)}) %all-reduce.6.cloned.1.call-update) | async-done | bytes 131088 | tf_op jit(solution)/shard_map/psum | solution.py:81
  209.7 1.6 broadcast_divide_fusion
  (169 shorter events, 59.7 us)
Async XLA Ops:
  7.2 18.2 %copy-start = (f32[8,32768]{1,0:T(8,128)S(1)}, f32[8,32768]{1,0:T(8,128)}, u32[]{:S(2)}) copy-start(f32[8,32768]{1,0:T(8,128)} %param.5) | copy-start | bytes 3145732
  7.2 128.9 %reduce-scatter.2.cloned.1.call-start = ((), (), s32[]{:S(2)}) async-start(), calls=%async_computation.2 | async-start | bytes 655360 | tf_op jit(solution)/shard_map/reduce_scatter | solution.py:73
  8.4 17.0 %collective-permute-start = (f32[8,16384]{1,0:T(8,128)S(1)}, f32[8,16384]{1,0:T(8,128)}, u32[]{:S(2)}, u32[]{:S(2)}) collective-permute-start(f32[8,16384]{1,0:T(8,128)S(1)} %slice.11), channel_id=1, source_target_pairs={{4,0},{8,4},{12,8},{5,1},{9,5},{13,9},{6,2},{10,6},{14,10},{7,3},{... | collective-permute-start | bytes 1572872 | tf_op jit(solution)/shard_map/ppermute | solution.py:15
  29.0 84.6 %copy-start.4 = (s32[8]{0:T(128)S(1)}, s32[8]{0:T(128)}, u32[]{:S(2)}) copy-start(s32[8]{0:T(128)} %param.7) | copy-start | bytes 100
  29.0 90.6 %copy-start.5 = (u32[32]{0:T(128)S(1)}, u32[32]{0:T(128)}, u32[]{:S(2)}) copy-start(u32[32]{0:T(128)} %constant.88) | copy-start | bytes 388
  29.0 91.2 %copy-start.3 = (s32[8,2]{0,1:T(2,128)S(1)}, s32[8,2]{0,1:T(2,128)}, u32[]{:S(2)}) copy-start(s32[8,2]{0,1:T(2,128)} %param.6) | copy-start | bytes 196
  113.5 17.4 %copy-start.1 = (f32[8,16384]{1,0:T(8,128)}, f32[8,16384]{1,0:T(8,128)S(1)}, u32[]{:S(2)}) copy-start(f32[8,16384]{1,0:T(8,128)S(1)} %get-tuple-element.78) | copy-start | bytes 1572868
  113.6 61.7 %all-reduce.4.cloned.1.call-start = ((), (), s32[]{:S(2)}) async-start(), calls=%async_computation.1 | async-start | bytes 1048576 | tf_op jit(solution)/shard_map/pmax | solution.py:70
  131.0 78.8 %all-reduce.6.cloned.1.call-start = ((), (), s32[]{:S(2)}) async-start(), calls=%async_computation.3 | async-start | bytes 262144 | tf_op jit(solution)/shard_map/psum | solution.py:81
  137.0 74.4 %copy-start.2 = (f32[8,4096]{1,0:T(8,128)}, f32[8,4096]{1,0:T(8,128)S(1)}, u32[]{:S(2)}) copy-start(f32[8,4096]{1,0:T(8,128)S(1)} %broadcast_divide_fusion.1) | copy-start | bytes 393220
Sparse Core Ops, SparseCore 0:
  113.7 22.3 reduce-scatter.1
  138.4 36.8 all-reduce.3
  178.1 31.5 all-reduce.5
where the time goes:
time: 219 us; the launch traced here: 218 us
  waiting for transfers between devices  90.2 us (41%)
  matrix products  42.8 us (20%)
  local copies, waits for them, and re-layouts  40.5 us (18%)
  blocking collectives  15.9 us (7%)
  between operations  13.8 us (6%)
  other arithmetic  12 us (5%)
    pmax x1, waiting for transfers between devices, on_device(): peak_all = lax.pmax(peak_local, 'tm')  37.3 us
    psum x1, waiting for transfers between devices, on_device(): lax.psum((block_part, jnp.sum(onehot, axis=1)), ('chan', 'sub'))  32.9 us
    dynamic_update_slice x16, local copies, waits for them, and re-layouts, on_device(): peak_local, log_terms = lax.map(one_channel, (hop_rows, gap_mask))  19.5 us
    ppermute x1, waiting for transfers between devices, from_behind(): return lax.ppermute(x, axis, pairs)  14.9 us
    unnamed x1, blocking collectives  10 us
    slice x8, local copies, waits for them, and re-layouts, one_channel(): segments = jnp.concatenate([rows_here[:-1], rows_here[1:]], axis=-1)  9.22 us
    dot_general x8, matrix products, one_channel(): jnp.einsum('ska,aj->skj', imag_mid, section_two[0], precision=highest)  8.05 us
    dot_general x8, matrix products, one_channel(): jnp.einsum('ska,aj->skj', real_mid, section_two[0], precision=highest)  7.94 us
  transfers between devices with their start and end apart: 4, of which 4 were waited for; matrix products, arithmetic and copies ran while one was open for 3% of the time, Pallas kernels for 0%

commit v1 on v0

--- a/solution.py
+++ b/solution.py
@@ -78,7 +78,9 @@
         jnp.float32
     )
     block_part = jnp.dot(onehot, log_mean, precision=highest)
-    block_total, block_counts = lax.psum((block_part, jnp.sum(onehot, axis=1)), ("chan", "sub"))
+    block_total, block_counts = lax.psum(
+        lax.psum((block_part, jnp.sum(onehot, axis=1)), "sub"), "chan"
+    )
     block_mean = block_total / block_counts[:, None]
     return (peak_hold, log_mean, block_mean)
 

time: 219 us -> 229 us (1.046)
  waiting for transfers between devices: 90.2 us -> 99.4 us
    reduce_scatter x1, waiting for transfers between devices: 5.01 us -> 10.8 us  [on_device(): lax.psum_scatter(log_terms, 'tm', scatter_dimension=1, tiled=True)]
    pmax x1, waiting for transfers between devices: 37.3 us -> 42.1 us  [on_device(): peak_all = lax.pmax(peak_local, 'tm')]
    psum x1 -> x2, waiting for transfers between devices: 32.9 us -> 30.9 us  [the longest x1 21.9 us: on_device(): lax.psum(lax.psum((block_part, jnp.sum(onehot, axis=1)), 'sub'), 'chan')]
    psum x1 -> x2, blocking collectives: 5.9 us -> 7.37 us  [the longest x1 4.91 us: on_device(): lax.psum(lax.psum((block_part, jnp.sum(onehot, axis=1)), 'sub'), 'chan')]
  transfers between devices with their start and end apart: 4 -> 5, of which waited for: 4 -> 5; matrix products, arithmetic and copies ran while one was open for 3% -> 2% of each run, Pallas kernels for 0% -> 0%
where the time goes in v1:
time: 229 us
  waiting for transfers between devices  99.4 us (43%)
  matrix products  42.8 us (19%)
  local copies, waits for them, and re-layouts  40.5 us (18%)
  blocking collectives  17.5 us (8%)
  between operations  13.9 us (6%)
  other arithmetic  12 us (5%)
    pmax x1, waiting for transfers between devices, on_device(): peak_all = lax.pmax(peak_local, 'tm')  42.1 us
    psum x1, waiting for transfers between devices, on_device(): lax.psum(lax.psum((block_part, jnp.sum(onehot, axis=1)), 'sub'), 'chan')  21.9 us
    dynamic_update_slice x16, local copies, waits for them, and re-layouts, on_device(): peak_local, log_terms = lax.map(one_channel, (hop_rows, gap_mask))  19.5 us
    ppermute x1, waiting for transfers between devices, from_behind(): return lax.ppermute(x, axis, pairs)  14.9 us
    reduce_scatter x1, waiting for transfers between devices, on_device(): lax.psum_scatter(log_terms, 'tm', scatter_dimension=1, tiled=True)  10.8 us
    unnamed x1, blocking collectives  10.2 us
    slice x8, local copies, waits for them, and re-layouts, one_channel(): segments = jnp.concatenate([rows_here[:-1], rows_here[1:]], axis=-1)  9.22 us
    psum x1, waiting for transfers between devices, on_device(): lax.psum((block_part, jnp.sum(onehot, axis=1)), 'sub')  8.94 us
  transfers between devices with their start and end apart: 5, of which 5 were waited for; matrix products, arithmetic and copies ran while one was open for 2% of the time, Pallas kernels for 0%

profile of v1, /device:TPU:0, one launch (start us, length us, event | category | flops | bytes accessed | tf_op | source)
XLA Modules:
  0.0 228.8 jit_solution(11907317303194092478)
XLA Ops:
  7.2 1.2 slice.11
  8.4 1.3 collective-permute-start
  10.5 14.9 %collective-permute-done = f32[8,16384]{1,0:T(8,128)} collective-permute-done((f32[8,16384]{1,0:T(8,128)S(1)}, f32[8,16384]{1,0:T(8,128)}, u32[]{:S(2)}, u32[]{:S(2)}) %collective-permute-start) | collective-permute-done | bytes 524320 | tf_op jit(solution)/shard_map/ppermute | solution.py:15
  25.4 1.1 pad_maximum_fusion
  26.5 2.5 %reshape.43 = f32[8,3,16384]{2,1,0:T(4,128)} reshape(f32[8,49152]{1,0:T(8,128)S(1)} %pad_maximum_fusion) | data formatting | bytes 3145728 | tf_op jit(solution)/shard_map/reshape | solution.py:36
  29.0 84.5 %while.14 = (s32[]{:T(128)}, f32[8,16384]{1,0:T(8,128)S(1)}, f32[8,16384]{1,0:T(8,128)}, f32[8,3,16384]{2,1,0:T(4,128)}, s32[8,2]{1,0:T(8,128)S(1)}, /*index=5*/s32[]{:T(128)}, s32[]{:T(128)}, s32[]{}) while((s32[]{:T(128)}, f32[8,16384]{1,0:T(8,128)S(1)}, f32[8,16384]{1,0:T(8,128)}, f32[8,3,16384]{2,1,0:T(4,128)}, ...), condition=%wide.region_3.4_spmd.clone.clone, body=%wide.region_0.3_spmd.clone.clone.sunk | while | flops 608321536 | bytes 8388765 | solution.py:65
  29.0 1.2 constant_dynamic-slice_fusion.5
  37.1 1.9 dynamic_update_slice.14
  39.6 1.1 constant_dynamic-slice_fusion.5
  47.6 1.9 dynamic_update_slice.14
  50.2 1.1 constant_dynamic-slice_fusion.5
  57.1 1.0 multiply_reduce_fusion.3
  58.2 1.9 dynamic_update_slice.14
  60.7 1.1 constant_dynamic-slice_fusion.5
  68.7 1.9 dynamic_update_slice.14
  71.3 1.1 constant_dynamic-slice_fusion.5
  79.3 1.9 dynamic_update_slice.14
  81.9 1.1 constant_dynamic-slice_fusion.5
  89.9 1.9 dynamic_update_slice.14
  92.4 1.1 constant_dynamic-slice_fusion.5
  100.4 1.9 dynamic_update_slice.14
  103.0 1.1 constant_dynamic-slice_fusion.5
  111.0 1.9 dynamic_update_slice.14
  114.2 10.2 %all-reduce = f32[8,4]{0,1:T(4,128)S(1)} all-reduce(f32[8,4]{0,1:T(4,128)S(1)} %broadcast_in_dim.8), channel_id=3, replica_groups=mesh['grp'=2,'tm'=4,'chan'=2,'sub'=2] {'tm'}, use_global_device_ids=true, to_apply=%region_7.8.clone | all-reduce | flops 32 | bytes 256
  125.1 10.8 %reduce-scatter.2.cloned.1.call-done = f32[8,4096]{1,0:T(8,128)} async-done(((f32[8,16384]{1,0:T(8,128)}), f32[8,4096]{1,0:T(8,128)}) %reduce-scatter.2.cloned.1.call-update) | async-done | bytes 131088 | tf_op jit(solution)/shard_map/reduce_scatter | solution.py:73
  138.7 2.5 %psum.30 = f32[8]{0:T(128)S(1)} all-reduce(f32[8]{0:T(128)S(1)} %convert_reduce_fusion), channel_id=1, replica_groups=mesh['grp'=2,'tm'=4,'chan'=2,'sub'=2] {'sub'}, use_global_device_ids=true, to_apply=%region_11.12 | all-reduce | flops 8 | bytes 64 | tf_op jit(solution)/shard_map/psum | solution.py:82
  141.2 4.9 %psum.31 = f32[8]{0:T(128)S(1)} all-reduce(f32[8]{0:T(128)S(1)} %psum.30), channel_id=1, replica_groups=mesh['grp'=2,'tm'=4,'chan'=2,'sub'=2] {'chan'}, use_global_device_ids=true, to_apply=%region_12.13 | all-reduce | flops 8 | bytes 64 | tf_op jit(solution)/shard_map/psum | solution.py:81
  146.1 8.9 %all-reduce.7.cloned.1.call-done = f32[8,4096]{1,0:T(8,128)} async-done(((f32[8,4096]{1,0:T(8,128)}), f32[8,4096]{1,0:T(8,128)}) %all-reduce.7.cloned.1.call-update) | async-done | bytes 131088 | tf_op jit(solution)/shard_map/psum | solution.py:82
  155.0 42.1 %all-reduce.5.cloned.1.call-done = f32[8,16384]{1,0:T(8,128)} async-done(((f32[8,16384]{1,0:T(8,128)}), f32[8,16384]{1,0:T(8,128)}) %all-reduce.5.cloned.1.call-update) | async-done | bytes 524304 | tf_op jit(solution)/shard_map/pmax | solution.py:70
  197.1 1.6 constant_dynamic-slice_fusion.3
  198.7 21.9 %all-reduce.9.cloned.1.call-done = f32[8,4096]{1,0:T(8,128)} async-done(((f32[8,4096]{1,0:T(8,128)}), f32[8,4096]{1,0:T(8,128)}) %all-reduce.9.cloned.1.call-update) | async-done | bytes 131088 | tf_op jit(solution)/shard_map/psum | solution.py:81
  220.6 1.6 broadcast_divide_fusion
  (173 shorter events, 62.5 us)
Async XLA Ops:
  7.2 18.2 %copy-start = (f32[8,32768]{1,0:T(8,128)S(1)}, f32[8,32768]{1,0:T(8,128)}, u32[]{:S(2)}) copy-start(f32[8,32768]{1,0:T(8,128)} %param.5) | copy-start | bytes 3145732
  7.2 128.7 %reduce-scatter.2.cloned.1.call-start = ((), (), s32[]{:S(2)}) async-start(), calls=%async_computation.2 | async-start | bytes 655360 | tf_op jit(solution)/shard_map/reduce_scatter | solution.py:73
  8.4 17.0 %collective-permute-start = (f32[8,16384]{1,0:T(8,128)S(1)}, f32[8,16384]{1,0:T(8,128)}, u32[]{:S(2)}, u32[]{:S(2)}) collective-permute-start(f32[8,16384]{1,0:T(8,128)S(1)} %slice.11), channel_id=1, source_target_pairs={{4,0},{8,4},{12,8},{5,1},{9,5},{13,9},{6,2},{10,6},{14,10},{7,3},{... | collective-permute-start | bytes 1572872 | tf_op jit(solution)/shard_map/ppermute | solution.py:15
  29.0 84.6 %copy-start.5 = (u32[32]{0:T(128)S(1)}, u32[32]{0:T(128)}, u32[]{:S(2)}) copy-start(u32[32]{0:T(128)} %constant.88) | copy-start | bytes 388
  29.0 85.2 %copy-start.3 = (s32[8,2]{0,1:T(2,128)S(1)}, s32[8,2]{0,1:T(2,128)}, u32[]{:S(2)}) copy-start(s32[8,2]{0,1:T(2,128)} %param.6) | copy-start | bytes 196
  29.0 107.9 %copy-start.4 = (s32[8]{0:T(128)S(1)}, s32[8]{0:T(128)}, u32[]{:S(2)}) copy-start(s32[8]{0:T(128)} %param.7) | copy-start | bytes 100
  113.5 24.3 %copy-start.1 = (f32[8,16384]{1,0:T(8,128)}, f32[8,16384]{1,0:T(8,128)S(1)}, u32[]{:S(2)}) copy-start(f32[8,16384]{1,0:T(8,128)S(1)} %get-tuple-element.78) | copy-start | bytes 1572868
  113.6 41.4 %all-reduce.7.cloned.1.call-start = ((), (), s32[]{:S(2)}) async-start(), calls=%async_computation.3 | async-start | bytes 262144 | tf_op jit(solution)/shard_map/psum | solution.py:82
  136.9 85.3 %copy-start.2 = (f32[8,4096]{1,0:T(8,128)}, f32[8,4096]{1,0:T(8,128)S(1)}, u32[]{:S(2)}) copy-start(f32[8,4096]{1,0:T(8,128)S(1)} %broadcast_divide_fusion.1) | copy-start | bytes 393220
  137.8 59.3 %all-reduce.5.cloned.1.call-start = ((), (), s32[]{:S(2)}) async-start(), calls=%async_computation.1 | async-start | bytes 1048576 | tf_op jit(solution)/shard_map/pmax | solution.py:70
  138.5 82.1 %all-reduce.9.cloned.1.call-start = ((), (), s32[]{:S(2)}) async-start(), calls=%async_computation.4 | async-start | bytes 262144 | tf_op jit(solution)/shard_map/psum | solution.py:81
Sparse Core Ops, SparseCore 0:
  113.7 22.1 reduce-scatter.1
  138.8 16.1 all-reduce.6
  157.3 39.7 all-reduce.4
  199.2 21.3 all-reduce.8
